TPU v7x, 128 devices: a whole 4x4x4 slice. The times are simulated.
128 devices in a mesh: res: 32 (over x_lo, y, z), seq: 4 (over x_hi, core).
Axes of the slice: x: 4 (x_hi: 2, x_lo: 2; x = x_hi * 2 + x_lo), y: 4, z: 4, core: 2. Of those that a mesh axis runs over, the one named last changes fastest.
Arguments:
- alignment: bfloat16 [384, 1024, 256], P('seq', 'res'), may hold values from -6 to 6
- query_weight: bfloat16 [256, 256], replicated, may hold values from -1 to 1
- w_keyval: bfloat16 [256, 512], replicated, may hold values from -0.375 to 0.375
- w_gate: bfloat16 [256, 256], replicated, may hold values from -0.375 to 0.375
- output_weight: bfloat16 [256, 256], replicated, may hold values from -0.75 to 0.75
- w_factors: bfloat16 [256, 64], replicated, may hold values from -1.5 to 1.5
- w_pair_out: bfloat16 [1024, 128], replicated, may hold values from -0.1875 to 0.1875
Outputs:
- alignment_update: bfloat16 [384, 1024, 256], P('seq', 'res')
- pair_representation_update: bfloat16 [1024, 1024, 128], P(('res', 'seq'))
All inputs are finite; a program needn't handle non-finite values.
Results may differ from a plain program's by a relative error of at most 0.012.
The roundings to bfloat16 on the way count: a program that leaves them out, or rounds other values in their place, can miss the bound.
Values may be sent and summed in bfloat16 or wider, within the bound.
A program may use at most 256 MiB of HBM per device.

v0:
```python
import math

import jax
import jax.numpy as jnp
from jax import lax
from jax.experimental import pallas as pl
from jax.experimental.pallas import tpu as pltpu
from jax.sharding import Mesh
from jax.sharding import PartitionSpec as P

HEADS = 8
HC = 32
C = 32
AXES = ("x_lo", "y", "z", "x_hi", "core")
SIZES = (2, 4, 4, 2, 2)
RES = ("x_lo", "y", "z")
SEQ = ("x_hi", "core")
epsilon = 1e-05
NT = (((1,), (1,)), ((), ()))
TN = (((0,), (0,)), ((), ()))
RELS = ((0, 0), (0, 1), (1, 0), (1, 1))
CHUNKS = 4
PER_CHUNK = 8 // CHUNKS
F32 = jnp.float32
BF16 = jnp.bfloat16
VMEM_SPEC = pl.BlockSpec(memory_space=pltpu.VMEM)
ANY_SPEC = pl.BlockSpec(memory_space=pl.ANY)
MESH = pl.DeviceIdType.MESH


def flipped(value, flip):
    return 1 - value if flip else value


def seq_of(rel):
    hi, core = lax.axis_index("x_hi"), lax.axis_index("core")
    return flipped(hi, RELS[rel][0]) * 2 + flipped(core, RELS[rel][1])


def seq_device(rel):
    hi, core = lax.axis_index("x_hi"), lax.axis_index("core")
    return {"x_hi": flipped(hi, RELS[rel][0]), "core": flipped(core, RELS[rel][1])}


def x_device(shift):
    x = lax.axis_index("x_hi") * 2 + lax.axis_index("x_lo")
    there = lax.rem(x + shift + 4, 4)
    return {"x_lo": lax.rem(there, 2), "x_hi": there // 2}


def y_device(shift):
    return {"y": lax.rem(lax.axis_index("y") + shift + 4, 4)}


def z_device(shift, flip):
    there = lax.rem(lax.axis_index("z") + shift + 4, 4)
    return {"z": there, "core": flipped(lax.axis_index("core"), flip)}


def remote(src, dst, send, recv, device):
    return pltpu.make_async_remote_copy(
        src_ref=src, dst_ref=dst, send_sem=send, recv_sem=recv, device_id=device, device_id_type=MESH
    )


def step_kernel(
    x_ref, wf_ref, wq_ref, wkv_ref, wg_ref, wo_ref, wp_ref,
    update_out, pair_out,
    normed_out, rows_in, factors_out, factors_in, rights, lefts, spread_q, w_turned, w_pair,
    update_made, aligned, held, blocks,
    f_send, f_recv, n_send, n_recv, x_send, x_recv, y_send, y_recv, w_send, w_recv,
    l_send, l_recv, u_send, u_recv, p_send, p_recv, own_sem,
):
    barrier = pltpu.get_barrier_semaphore()
    partners = [seq_device(rel) for rel in (1, 2, 3)] + [x_device(1), x_device(-1)]
    partners += [y_device(1), y_device(-1)]
    partners += [z_device(dz, dc) for dz in (1, 2, 3) for dc in (0, 1)]
    for device in partners:
        pl.semaphore_signal(barrier, inc=1, device_id=device, device_id_type=MESH)

    def factor_copy(rel):
        return remote(
            factors_out.at[rel - 1], factors_in.at[seq_of(0)],
            f_send.at[rel - 1], f_recv.at[rel - 1], seq_device(rel),
        )

    def normed_copy(rel, chunk):
        part = pl.ds(chunk * PER_CHUNK, PER_CHUNK)
        return remote(
            normed_out.at[rel - 1, part], rows_in.at[rel, part],
            n_send.at[rel - 1, chunk], n_recv.at[rel - 1, chunk], seq_device(rel),
        )

    def x_copy(dx):
        return remote(
            rights.at[0, 0], rights.at[0, dx], x_send.at[dx - 1], x_recv.at[dx - 1], x_device(-dx)
        )

    def y_copy(dx, way):
        return remote(
            rights.at[0, dx], rights.at[(1, 3)[way], dx],
            y_send.at[dx, way], y_recv.at[dx, way], y_device((-1, 1)[way]),
        )

    def relay_copy(dx, way):
        half = pl.ds(16 * way, 16)
        return remote(
            rights.at[(1, 3)[way], dx, half], rights.at[2, dx, half],
            w_send.at[dx, way], w_recv.at[dx, way], y_device((-1, 1)[way]),
        )

    def left_copy(n):
        dz, dc = n // 2, n % 2
        return remote(
            lefts.at[0, 0], lefts.at[dz, dc], l_send.at[n - 1], l_recv.at[n - 1], z_device(-dz, dc)
        )

    def update_copy(rel, chunk):
        part = pl.ds(chunk * PER_CHUNK, PER_CHUNK)
        return remote(
            update_made.at[rel, part], update_out.at[rel, part],
            u_send.at[rel - 1, chunk], u_recv.at[rel - 1, chunk], seq_device(rel),
        )

    def block_copy(n):
        dz, dc = n // 2, n % 2
        there = 2 * ((4 - dz) % 4) + dc
        return remote(
            blocks.at[n], pair_out.at[there], p_send.at[n - 1], p_recv.at[there - 1],
            z_device(dz, dc),
        )

    weight = wf_ref[...]
    none = jnp.zeros_like(weight)
    even = jnp.concatenate([weight, none], axis=0)
    odd = jnp.concatenate([none, weight], axis=0)
    span = 32
    for rel in (1, 2, 3, 0):
        first = pl.multiple_of(seq_of(rel) * 8, 8)
        normed_ref = normed_out.at[rel - 1] if rel else rows_in.at[0]
        factor_ref = factors_out.at[rel - 1] if rel else factors_in.at[seq_of(0)]

        def norm_rows(part, _, first=first, normed_ref=normed_ref):
            rows = pl.ds(pl.multiple_of(part * span, span), span)
            x = x_ref[rows, pl.ds(first, 8), :].astype(F32)
            centered = x - jnp.mean(x, axis=-1, keepdims=True)
            spread = jnp.mean(centered * centered, axis=-1, keepdims=True)
            normed = centered * lax.rsqrt(spread + epsilon)
            normed_ref[:, rows, :] = jnp.swapaxes(normed, 0, 1).astype(BF16)
            return 0

        lax.fori_loop(0, 96 // span, norm_rows, 0, unroll=True)
        for pair in range(4):
            made = lax.dot_general(
                normed_ref[2 * pair], even, NT, preferred_element_type=F32
            ) + lax.dot_general(normed_ref[2 * pair + 1], odd, NT, preferred_element_type=F32)
            factor_ref[:, pair * 128 : (pair + 1) * 128] = made.astype(BF16)
        if rel == 1:
            pl.semaphore_wait(barrier, len(partners))
        if rel:
            factor_copy(rel).start()
    for rel in (1, 2, 3):
        normed_copy(rel, 0).start()

    w_turned[:256] = wq_ref[...].astype(F32).T.astype(BF16)
    w_turned[256:512] = wkv_ref[:, 256:].astype(F32).T.astype(BF16)
    w_turned[512:] = wg_ref[...].astype(F32).T.astype(BF16)
    pair_rows = jnp.swapaxes(wp_ref[...].astype(F32).reshape(C, C, 128), 0, 1)
    w_pair[...] = pair_rows.reshape(C * C, 128).T.astype(BF16)
    spread_q[...] = jnp.zeros_like(spread_q)

    for rel in (1, 2, 3):
        factor_copy(rel).wait_recv()
    turned = factors_in[...].astype(F32).reshape(384, 512).T.reshape(8, 64, 384)
    rights[0, 0] = jnp.swapaxes(turned[:, C:], 0, 1).astype(BF16)
    lefts[0, 0] = turned[:, :C].reshape(8 * C, 384).astype(BF16)
    for dx in (1, 3, 2):
        x_copy(dx).start()
    for way in (0, 1):
        y_copy(0, way).start()
    for n in range(1, 8):
        left_copy(n).start()
    for chunk in range(1, CHUNKS):
        for rel in (1, 2, 3):
            normed_copy(rel, chunk).start()

    ones = jnp.ones((16, 384), BF16)
    scale = 1.0 / math.sqrt(HC)

    def residue(r, _):
        rows = jnp.concatenate([rows_in[k, r] for k in range(4)], axis=0)
        keys = jnp.dot(rows, wkv_ref[:, :256], preferred_element_type=F32).astype(BF16)
        queries = lax.dot_general(w_turned[:256], rows, NT, preferred_element_type=F32).astype(BF16)
        values = lax.dot_general(
            w_turned[256:512], rows, NT, preferred_element_type=F32
        ).astype(BF16)
        gating = jax.nn.sigmoid(
            lax.dot_general(w_turned[512:], rows, NT, preferred_element_type=F32)
        )
        for h in range(HEADS):
            at = slice(h * HC, (h + 1) * HC)
            spread_q[h // 2, at, (h % 2) * 384 : (h % 2 + 1) * 384] = queries[at]
        gated = []
        for pair in range(HEADS // 2):
            scores = jnp.dot(keys, spread_q[pair], preferred_element_type=F32)
            weights = jnp.exp(scores * scale).astype(BF16)
            for k in range(2):
                h = 2 * pair + k
                at = slice(h * HC, (h + 1) * HC)
                summed = jnp.dot(
                    jnp.concatenate([values[at], ones], axis=0),
                    weights[:, k * 384 : (k + 1) * 384],
                    preferred_element_type=F32,
                )
                attended = summed[:HC] / summed[HC : HC + 1]
                gated.append((gating[at] * attended).astype(BF16))
        update = lax.dot_general(
            jnp.concatenate(gated, axis=0), wo_ref[...], TN, preferred_element_type=F32
        ).astype(BF16)
        for k in range(4):
            update_made[k, r] = update[k * 96 : (k + 1) * 96]
        return 0

    def chunk_step(chunk, _):
        for rel in (1, 2, 3):
            normed_copy(rel, chunk).wait_recv()
        lax.fori_loop(chunk * PER_CHUNK, (chunk + 1) * PER_CHUNK, residue, 0)
        for rel in (1, 2, 3):
            update_copy(rel, chunk).start()

        @pl.when(chunk == 0)
        def _():
            for dx in (1, 3):
                x_copy(dx).wait_recv()
                for way in (0, 1):
                    y_copy(dx, way).start()
            for way in (0, 1):
                y_copy(0, way).wait_recv()
                relay_copy(0, way).start()
            x_copy(2).wait_recv()
            for way in (0, 1):
                y_copy(2, way).start()

        @pl.when(chunk == 1)
        def _():
            for dx in (1, 3):
                for way in (0, 1):
                    y_copy(dx, way).wait_recv()
                    relay_copy(dx, way).start()

        @pl.when(chunk == 2)
        def _():
            for way in (0, 1):
                y_copy(2, way).wait_recv()
                relay_copy(2, way).start()

        return 0

    lax.fori_loop(0, CHUNKS, chunk_step, 0)

    own_update = pltpu.make_async_copy(update_made.at[0], update_out.at[0], own_sem.at[0])
    own_update.start()

    for dx in range(4):
        for way in (0, 1):
            relay_copy(dx, way).wait_recv()

    def align(e, _):
        aligned[e] = jnp.concatenate(
            [rights[dy, dx, e] for dy in range(4) for dx in range(4)], axis=0
        )
        return 0

    lax.fori_loop(0, C, align, 0)
    for n in range(1, 8):
        left_copy(n).wait_recv()

    for dz in (2, 1, 3, 0):
        left = lefts.at[dz]

        def products(k, _, left=left):
            right = aligned[pl.ds(2 * k, 2)].reshape(256, 384)
            made = lax.dot_general(
                left[...].reshape(512, 384), right, NT, preferred_element_type=F32
            ).astype(BF16)
            for e in range(2):
                at = pl.multiple_of((2 * k + e) * C, C)
                held[:, pl.ds(at, C), :] = made[:, e * 128 : (e + 1) * 128].reshape(16, C, 128)
            return 0

        lax.fori_loop(0, C // 2, products, 0)
        for dc in (0, 1):

            def project(pair, _, dz=dz, dc=dc):
                i = 8 * dc + 2 * pair
                cols = jnp.concatenate([held[i], held[i + 1]], axis=1)
                made = jnp.dot(w_pair[...], cols, preferred_element_type=F32) * (1.0 / 384)
                for k in range(2):
                    blocks[2 * dz + dc, 2 * pair + k] = (
                        made[:, k * 128 : (k + 1) * 128].T.astype(BF16)
                    )
                return 0

            lax.fori_loop(0, 4, project, 0)
            if dz or dc:
                block_copy(2 * dz + dc).start()
    own_block = pltpu.make_async_copy(blocks.at[0], pair_out.at[0], own_sem.at[1])
    own_block.start()

    for rel in (1, 2, 3):
        factor_copy(rel).wait_send()
        for chunk in range(CHUNKS):
            normed_copy(rel, chunk).wait_send()
            update_copy(rel, chunk).wait()
    for dx in (1, 2, 3):
        x_copy(dx).wait_send()
    for dx in range(4):
        for way in (0, 1):
            y_copy(dx, way).wait_send()
            relay_copy(dx, way).wait_send()
    for n in range(1, 8):
        left_copy(n).wait_send()
    own_update.wait()
    own_block.wait()
    for n in range(1, 8):
        block_copy(n).wait()


def step_call(alignment, w_factors, query_weight, w_keyval, w_gate, output_weight, w_pair_out):
    dma = pltpu.SemaphoreType.DMA
    return pl.pallas_call(
        step_kernel,
        in_specs=[VMEM_SPEC] * 7,
        out_specs=[ANY_SPEC] * 2,
        out_shape=[
            jax.ShapeDtypeStruct((4, 8, 96, 256), BF16),
            jax.ShapeDtypeStruct((8, 8, 128, 128), BF16),
        ],
        scratch_shapes=[
            pltpu.VMEM((3, 8, 96, 256), BF16),
            pltpu.VMEM((4, 8, 96, 256), BF16),
            pltpu.VMEM((3, 96, 512), BF16),
            pltpu.VMEM((4, 96, 512), BF16),
            pltpu.VMEM((4, 4, C, 8, 384), BF16),
            pltpu.VMEM((4, 2, 8 * C, 384), BF16),
            pltpu.VMEM((4, 256, 768), BF16),
            pltpu.VMEM((768, 256), BF16),
            pltpu.VMEM((128, C * C), BF16),
            pltpu.VMEM((4, 8, 96, 256), BF16),
            pltpu.VMEM((C, 128, 384), BF16),
            pltpu.VMEM((16, C * C, 128), BF16),
            pltpu.VMEM((8, 8, 128, 128), BF16),
            dma((3,)), dma((3,)), dma((3, CHUNKS)), dma((3, CHUNKS)), dma((3,)), dma((3,)),
            dma((4, 2)), dma((4, 2)), dma((4, 2)), dma((4, 2)), dma((7,)), dma((7,)),
            dma((3, CHUNKS)), dma((3, CHUNKS)), dma((7,)), dma((7,)), dma((2,)),
        ],
        compiler_params=pltpu.CompilerParams(
            collective_id=0, has_side_effects=True, vmem_limit_bytes=58 * 2**20
        ),
        name="step",
    )(alignment, w_factors.T, query_weight, w_keyval, w_gate, output_weight, w_pair_out)


def place_update_kernel(parts, out_ref, turned, sems):
    copies = []
    for rel in range(4):
        turned[rel] = jnp.swapaxes(parts[rel].astype(F32), 0, 1).astype(BF16)
        first = pl.multiple_of(seq_of(rel) * 8, 8)
        copy = pltpu.make_async_copy(
            turned.at[rel], out_ref.at[:, pl.ds(first, 8), :], sems.at[rel]
        )
        copy.start()
        copies.append(copy)
    for copy in copies:
        copy.wait()


def place_update(parts):
    return pl.pallas_call(
        place_update_kernel,
        in_specs=[VMEM_SPEC],
        out_specs=ANY_SPEC,
        out_shape=jax.ShapeDtypeStruct((96, 32, 256), BF16),
        scratch_shapes=[
            pltpu.VMEM((4, 96, 8, 256), BF16),
            pltpu.SemaphoreType.DMA((4,)),
        ],
        name="place_update",
    )(parts)


def place_pair_kernel(parts, out_ref, sem):
    x = lax.axis_index("x_hi") * 2 + lax.axis_index("x_lo")
    y, z, core = lax.axis_index("y"), lax.axis_index("z"), lax.axis_index("core")
    copies = []
    for n in range(8):
        there_z, there_core = lax.rem(z + n // 2, 4), flipped(core, n % 2)
        for dy in range(4):
            there_y = lax.rem(y + dy, 4)
            for dx in range(4):
                there_x = lax.rem(x + dx, 4)
                copy = pltpu.make_async_copy(
                    parts.at[n, :, dy * 4 + dx],
                    out_ref.at[
                        :, lax.rem(there_x, 2), there_y, there_z, there_x // 2, there_core
                    ],
                    sem,
                )
                copy.start()
                copies.append(copy)
    for copy in copies:
        copy.wait()


def place_pair(parts):
    made = pl.pallas_call(
        place_pair_kernel,
        in_specs=[VMEM_SPEC],
        out_specs=ANY_SPEC,
        out_shape=jax.ShapeDtypeStruct((8, 2, 4, 4, 2, 2, 8, 128), BF16),
        scratch_shapes=[pltpu.SemaphoreType.DMA],
        name="place_pair",
    )(parts.reshape(8, 8, 16, 8, 128))
    return made.reshape(8, 1024, 128)


def per_device(alignment, query_weight, w_keyval, w_gate, output_weight, w_factors, w_pair_out):
    update, pieces = step_call(
        alignment, w_factors, query_weight, w_keyval, w_gate, output_weight, w_pair_out
    )
    return (place_update(update), place_pair(pieces))


def solution(mesh):
    split = Mesh(mesh.devices.reshape(SIZES), AXES)
    in_specs = (P(SEQ, RES, None), P(), P(), P(), P(), P(), P())
    out_specs = (P(SEQ, RES, None), P(AXES, None, None))
    return jax.shard_map(
        per_device, mesh=split, in_specs=in_specs, out_specs=out_specs, check_vma=False
    )
```

profile of v0, /device:TPU:1, one launch (start us, length us, event | category | flops | bytes accessed | tf_op | source)
XLA Modules:
  0.0 92.7 jit_solution(17142495725979367243)
XLA Ops:
  0.6 86.3 %step.1 = (bf16[4,8,96,256]{3,2,1,0:T(8,128)(2,1)}, bf16[8,8,128,128]{3,2,1,0:T(8,128)(2,1)}) custom-call(bf16[96,32,256]{2,1,0:T(8,128)(2,1)} %x_ref.1, bf16[64,256]{1,0:T(8,128)(2,1)} %bitcast.5, bf16[256,256]{1,0:T(8,128)(2,1)} %wq_ref.1, bf16[256,512]{1,0:T(8,128)(2,1)} %wkv_ref.1, bf16[256,256]{1,0:T(8,128)(2,1)} %wg_ref.1, bf16[256,256]{1,0:T(8,128)(2,1)} %wo_ref.1, ...), custom_call_target="tpu_custom_call" | custom-call | tf_op jit(solution)/shard_map/step/pallas_call | solution.py:331
  86.9 2.9 %place_update.1 = bf16[96,32,256]{2,1,0:T(8,128)(2,1)} custom-call(bf16[4,8,96,256]{3,2,1,0:T(8,128)(2,1)} %get-tuple-element.4.parts), custom_call_target="tpu_custom_call" | custom-call | tf_op jit(solution)/shard_map/place_update/pallas_call | solution.py:379
  89.8 2.9 %place_pair.1 = bf16[8,2,4,4,2,2,8,128]{7,6,5,4,3,2,1,0:T(8,128)(2,1)} custom-call(bf16[8,8,16,8,128]{4,3,2,1,0:T(8,128)(2,1)} %bitcast.4), custom_call_target="tpu_custom_call" | custom-call | tf_op jit(solution)/shard_map/place_pair/pallas_call | solution.py:416
where the time goes:
time: 92.9 us; the launch traced here: 92.7 us
  Pallas kernels  92 us (99%)
    pallas_call x1, Pallas kernels, step_call(): pl.pallas_call(step_kernel, in_specs=[VMEM_SPEC] * 7, out_specs=[ANY_SPEC...  86.3 us
    pallas_call x1, Pallas kernels, place_pair(): pl.pallas_call(place_pair_kernel, in_specs=[VMEM_SPEC], out_specs=ANY_SPE...  2.87 us
    pallas_call x1, Pallas kernels, place_update(): pl.pallas_call(place_update_kernel, in_specs=[VMEM_SPEC], out_specs=ANY_S...  2.86 us

commit v1 on v0

--- a/solution.py
+++ b/solution.py
@@ -48,13 +48,22 @@
     return {"x_lo": lax.rem(there, 2), "x_hi": there // 2}
 
 
-def y_device(shift):
-    return {"y": lax.rem(lax.axis_index("y") + shift + 4, 4)}
-
-
-def z_device(shift, flip):
-    there = lax.rem(lax.axis_index("z") + shift + 4, 4)
-    return {"z": there, "core": flipped(lax.axis_index("core"), flip)}
+def gather_device(shift, flip=0):
+    core = lax.axis_index("core")
+    return {
+        "y": lax.rem(lax.axis_index("y") + (1 - core) * (shift + 4), 4),
+        "z": lax.rem(lax.axis_index("z") + core * (shift + 4), 4),
+        "core": flipped(core, flip),
+    }
+
+
+def share_device(shift, flip=0):
+    core = lax.axis_index("core")
+    return {
+        "y": lax.rem(lax.axis_index("y") + core * (shift + 4), 4),
+        "z": lax.rem(lax.axis_index("z") + (1 - core) * (shift + 4), 4),
+        "core": flipped(core, flip),
+    }
 
 
 def remote(src, dst, send, recv, device):
@@ -73,8 +82,9 @@
 ):
     barrier = pltpu.get_barrier_semaphore()
     partners = [seq_device(rel) for rel in (1, 2, 3)] + [x_device(1), x_device(-1)]
-    partners += [y_device(1), y_device(-1)]
-    partners += [z_device(dz, dc) for dz in (1, 2, 3) for dc in (0, 1)]
+    partners += [gather_device(1), gather_device(-1)]
+    partners += [share_device(shift, flip) for shift in (1, 2, 3) for flip in (0, 1)]
+    partners += [gather_device(shift, 1) for shift in (1, 2, 3)]
     for device in partners:
         pl.semaphore_signal(barrier, inc=1, device_id=device, device_id_type=MESH)
 
@@ -99,20 +109,21 @@
     def y_copy(dx, way):
         return remote(
             rights.at[0, dx], rights.at[(1, 3)[way], dx],
-            y_send.at[dx, way], y_recv.at[dx, way], y_device((-1, 1)[way]),
+            y_send.at[dx, way], y_recv.at[dx, way], gather_device((-1, 1)[way]),
         )
 
     def relay_copy(dx, way):
         half = pl.ds(16 * way, 16)
         return remote(
             rights.at[(1, 3)[way], dx, half], rights.at[2, dx, half],
-            w_send.at[dx, way], w_recv.at[dx, way], y_device((-1, 1)[way]),
+            w_send.at[dx, way], w_recv.at[dx, way], gather_device((-1, 1)[way]),
         )
 
     def left_copy(n):
-        dz, dc = n // 2, n % 2
-        return remote(
-            lefts.at[0, 0], lefts.at[dz, dc], l_send.at[n - 1], l_recv.at[n - 1], z_device(-dz, dc)
+        away, flip = n // 2, n % 2
+        device = gather_device(-away, 1) if flip else share_device(-away)
+        return remote(
+            lefts.at[0, 0], lefts.at[away, flip], l_send.at[n - 1], l_recv.at[n - 1], device
         )
 
     def update_copy(rel, chunk):
@@ -127,7 +138,7 @@
         there = 2 * ((4 - dz) % 4) + dc
         return remote(
             blocks.at[n], pair_out.at[there], p_send.at[n - 1], p_recv.at[there - 1],
-            z_device(dz, dc),
+            share_device(dz, dc),
         )
 
     weight = wf_ref[...]
@@ -135,7 +146,7 @@
     even = jnp.concatenate([weight, none], axis=0)
     odd = jnp.concatenate([none, weight], axis=0)
     span = 32
-    for rel in (1, 2, 3, 0):
+    for rel in (2, 3, 1, 0):
         first = pl.multiple_of(seq_of(rel) * 8, 8)
         normed_ref = normed_out.at[rel - 1] if rel else rows_in.at[0]
         factor_ref = factors_out.at[rel - 1] if rel else factors_in.at[seq_of(0)]
@@ -155,7 +166,7 @@
                 normed_ref[2 * pair], even, NT, preferred_element_type=F32
             ) + lax.dot_general(normed_ref[2 * pair + 1], odd, NT, preferred_element_type=F32)
             factor_ref[:, pair * 128 : (pair + 1) * 128] = made.astype(BF16)
-        if rel == 1:
+        if rel == 2:
             pl.semaphore_wait(barrier, len(partners))
         if rel:
             factor_copy(rel).start()
@@ -185,9 +196,9 @@
             normed_copy(rel, chunk).start()
 
     ones = jnp.ones((16, 384), BF16)
-    scale = 1.0 / math.sqrt(HC)
-
-    def residue(r, _):
+    scale = math.log2(math.e) / math.sqrt(HC)
+
+    def residue(r, slot):
         rows = jnp.concatenate([rows_in[k, r] for k in range(4)], axis=0)
         keys = jnp.dot(rows, wkv_ref[:, :256], preferred_element_type=F32).astype(BF16)
         queries = lax.dot_general(w_turned[:256], rows, NT, preferred_element_type=F32).astype(BF16)
@@ -199,11 +210,11 @@
         )
         for h in range(HEADS):
             at = slice(h * HC, (h + 1) * HC)
-            spread_q[h // 2, at, (h % 2) * 384 : (h % 2 + 1) * 384] = queries[at]
+            spread_q[slot, h // 2, at, (h % 2) * 384 : (h % 2 + 1) * 384] = queries[at]
         gated = []
         for pair in range(HEADS // 2):
-            scores = jnp.dot(keys, spread_q[pair], preferred_element_type=F32)
-            weights = jnp.exp(scores * scale).astype(BF16)
+            scores = jnp.dot(keys, spread_q[slot, pair], preferred_element_type=F32)
+            weights = jnp.exp2(scores * scale).astype(BF16)
             for k in range(2):
                 h = 2 * pair + k
                 at = slice(h * HC, (h + 1) * HC)
@@ -219,12 +230,12 @@
         ).astype(BF16)
         for k in range(4):
             update_made[k, r] = update[k * 96 : (k + 1) * 96]
-        return 0
 
     def chunk_step(chunk, _):
         for rel in (1, 2, 3):
             normed_copy(rel, chunk).wait_recv()
-        lax.fori_loop(chunk * PER_CHUNK, (chunk + 1) * PER_CHUNK, residue, 0)
+        for k in range(PER_CHUNK):
+            residue(chunk * PER_CHUNK + k, k)
         for rel in (1, 2, 3):
             update_copy(rel, chunk).start()
 
@@ -271,7 +282,7 @@
         )
         return 0
 
-    lax.fori_loop(0, C, align, 0)
+    lax.fori_loop(0, C, align, 0, unroll=4)
     for n in range(1, 8):
         left_copy(n).wait_recv()
 
@@ -288,7 +299,7 @@
                 held[:, pl.ds(at, C), :] = made[:, e * 128 : (e + 1) * 128].reshape(16, C, 128)
             return 0
 
-        lax.fori_loop(0, C // 2, products, 0)
+        lax.fori_loop(0, C // 2, products, 0, unroll=4)
         for dc in (0, 1):
 
             def project(pair, _, dz=dz, dc=dc):
@@ -301,7 +312,7 @@
                     )
                 return 0
 
-            lax.fori_loop(0, 4, project, 0)
+            lax.fori_loop(0, 4, project, 0, unroll=True)
             if dz or dc:
                 block_copy(2 * dz + dc).start()
     own_block = pltpu.make_async_copy(blocks.at[0], pair_out.at[0], own_sem.at[1])
@@ -343,7 +354,7 @@
             pltpu.VMEM((4, 96, 512), BF16),
             pltpu.VMEM((4, 4, C, 8, 384), BF16),
             pltpu.VMEM((4, 2, 8 * C, 384), BF16),
-            pltpu.VMEM((4, 256, 768), BF16),
+            pltpu.VMEM((PER_CHUNK, 4, 256, 768), BF16),
             pltpu.VMEM((768, 256), BF16),
             pltpu.VMEM((128, C * C), BF16),
             pltpu.VMEM((4, 8, 96, 256), BF16),
@@ -361,74 +372,81 @@
     )(alignment, w_factors.T, query_weight, w_keyval, w_gate, output_weight, w_pair_out)
 
 
-def place_update_kernel(parts, out_ref, turned, sems):
-    copies = []
-    for rel in range(4):
-        turned[rel] = jnp.swapaxes(parts[rel].astype(F32), 0, 1).astype(BF16)
-        first = pl.multiple_of(seq_of(rel) * 8, 8)
-        copy = pltpu.make_async_copy(
-            turned.at[rel], out_ref.at[:, pl.ds(first, 8), :], sems.at[rel]
-        )
-        copy.start()
-        copies.append(copy)
-    for copy in copies:
-        copy.wait()
-
-
-def place_update(parts):
-    return pl.pallas_call(
-        place_update_kernel,
-        in_specs=[VMEM_SPEC],
-        out_specs=ANY_SPEC,
-        out_shape=jax.ShapeDtypeStruct((96, 32, 256), BF16),
-        scratch_shapes=[
-            pltpu.VMEM((4, 96, 8, 256), BF16),
-            pltpu.SemaphoreType.DMA((4,)),
-        ],
-        name="place_update",
-    )(parts)
-
-
-def place_pair_kernel(parts, out_ref, sem):
+def place_kernel(update_ref, pair_ref, update_out, pair_out, rows, turned, pieces, *sems):
+    row_sems, piece_sems, turned_sems, placed_sem = sems
     x = lax.axis_index("x_hi") * 2 + lax.axis_index("x_lo")
     y, z, core = lax.axis_index("y"), lax.axis_index("z"), lax.axis_index("core")
+    row_loads = [
+        pltpu.make_async_copy(update_ref.at[n], rows.at[n], row_sems.at[n]) for n in range(4)
+    ]
+    piece_loads = [
+        pltpu.make_async_copy(pair_ref.at[n], pieces.at[n], piece_sems.at[n]) for n in range(8)
+    ]
+    for load in row_loads + piece_loads:
+        load.start()
     copies = []
-    for n in range(8):
-        there_z, there_core = lax.rem(z + n // 2, 4), flipped(core, n % 2)
-        for dy in range(4):
-            there_y = lax.rem(y + dy, 4)
+
+    def put(piece):
+        there_core = flipped(core, piece % 2)
+        away = piece // 2
+        for step in range(4):
+            there_y = lax.rem(y + there_core * away + (1 - there_core) * step, 4)
+            there_z = lax.rem(z + there_core * step + (1 - there_core) * away, 4)
             for dx in range(4):
                 there_x = lax.rem(x + dx, 4)
                 copy = pltpu.make_async_copy(
-                    parts.at[n, :, dy * 4 + dx],
-                    out_ref.at[
+                    pieces.at[piece, :, step * 4 + dx],
+                    pair_out.at[
                         :, lax.rem(there_x, 2), there_y, there_z, there_x // 2, there_core
                     ],
-                    sem,
+                    placed_sem,
                 )
                 copy.start()
                 copies.append(copy)
+
+    for n in range(4):
+        row_loads[n].wait()
+        turned[n] = jnp.swapaxes(rows[n].astype(F32), 0, 1).astype(BF16)
+        first = pl.multiple_of(seq_of(n) * 8, 8)
+        copy = pltpu.make_async_copy(
+            turned.at[n], update_out.at[:, pl.ds(first, 8), :], turned_sems.at[n]
+        )
+        copy.start()
+        copies.append(copy)
+        for piece in (2 * n, 2 * n + 1):
+            piece_loads[piece].wait()
+            put(piece)
     for copy in copies:
         copy.wait()
 
 
-def place_pair(parts):
-    made = pl.pallas_call(
-        place_pair_kernel,
-        in_specs=[VMEM_SPEC],
-        out_specs=ANY_SPEC,
-        out_shape=jax.ShapeDtypeStruct((8, 2, 4, 4, 2, 2, 8, 128), BF16),
-        scratch_shapes=[pltpu.SemaphoreType.DMA],
-        name="place_pair",
-    )(parts.reshape(8, 8, 16, 8, 128))
-    return made.reshape(8, 1024, 128)
+def place_call(update, pieces):
+    dma = pltpu.SemaphoreType.DMA
+    update, pair = pl.pallas_call(
+        place_kernel,
+        in_specs=[ANY_SPEC] * 2,
+        out_specs=[ANY_SPEC] * 2,
+        out_shape=[
+            jax.ShapeDtypeStruct((96, 32, 256), BF16),
+            jax.ShapeDtypeStruct((8, 2, 4, 4, 2, 2, 8, 128), BF16),
+        ],
+        scratch_shapes=[
+            pltpu.VMEM((4, 8, 96, 256), BF16),
+            pltpu.VMEM((4, 96, 8, 256), BF16),
+            pltpu.VMEM((8, 8, 16, 8, 128), BF16),
+            dma((4,)), dma((8,)), dma((4,)), dma,
+        ],
+        compiler_params=pltpu.CompilerParams(vmem_limit_bytes=58 * 2**20),
+        name="place",
+    )(update, pieces.reshape(8, 8, 16, 8, 128))
+    return update, pair.reshape(8, 1024, 128)
 
 
 def per_device(alignment, query_weight, w_keyval, w_gate, output_weight, w_factors, w_pair_out):
     update, pieces = step_call(
         alignment, w_factors, query_weight, w_keyval, w_gate, output_weight, w_pair_out
     )
-    return (place_update(update), place_pair(pieces))
+    return place_call(update, pieces)
 
 
 def solution(mesh):

time: 92.9 us -> 72.2 us (0.78)
  Pallas kernels: 92 us -> 71.3 us
    pallas_call x1, Pallas kernels: 86.3 us -> 67.8 us  [step_call(): pl.pallas_call(step_kernel, in_specs=[VMEM_SPEC] * 7, out_specs=[ANY_SPEC...]
    pallas_call x2 -> x1, Pallas kernels: 5.73 us -> 3.46 us  [place_call(): pl.pallas_call(place_kernel, in_specs=[ANY_SPEC] * 2, out_specs=[ANY_SPEC...]
where the time goes in v1:
time: 72.2 us; the launch traced here: 72.1 us
  Pallas kernels  71.3 us (99%)
  between operations  0.8 us (1%)
    pallas_call x1, Pallas kernels, step_call(): pl.pallas_call(step_kernel, in_specs=[VMEM_SPEC] * 7, out_specs=[ANY_SPEC...  67.8 us
    pallas_call x1, Pallas kernels, place_call(): pl.pallas_call(place_kernel, in_specs=[ANY_SPEC] * 2, out_specs=[ANY_SPEC...  3.46 us

profile of v1, /device:TPU:1, one launch (start us, length us, event | category | flops | bytes accessed | tf_op | source)
XLA Modules:
  0.0 72.1 jit_solution(6802137741737115391)
XLA Ops:
  0.6 67.8 %step.1 = (bf16[4,8,96,256]{3,2,1,0:T(8,128)(2,1)}, bf16[8,8,128,128]{3,2,1,0:T(8,128)(2,1)}) custom-call(bf16[96,32,256]{2,1,0:T(8,128)(2,1)} %x_ref.1, bf16[64,256]{1,0:T(8,128)(2,1)} %bitcast.4, bf16[256,256]{1,0:T(8,128)(2,1)} %wq_ref.1, bf16[256,512]{1,0:T(8,128)(2,1)} %wkv_ref.1, bf16[256,256]{1,0:T(8,128)(2,1)} %wg_ref.1, bf16[256,256]{1,0:T(8,128)(2,1)} %wo_ref.1, ...), custom_call_target="tpu_custom_call" | custom-call | tf_op jit(solution)/shard_map/step/pallas_call | solution.py:342
  68.4 3.5 %place.1 = (bf16[96,32,256]{2,1,0:T(8,128)(2,1)}, bf16[8,2,4,4,2,2,8,128]{7,6,5,4,3,2,1,0:T(8,128)(2,1)}) custom-call(bf16[4,8,96,256]{3,2,1,0:T(8,128)(2,1)} %get-tuple-element.6.update_ref, bf16[8,8,16,8,128]{4,3,2,1,0:T(8,128)(2,1)} %bitcast.3), custom_call_target="tpu_custom_call" | custom-call | tf_op jit(solution)/shard_map/place/pallas_call | solution.py:425

commit v2 on v1

--- a/solution.py
+++ b/solution.py
@@ -73,13 +73,34 @@
 
 
 def step_kernel(
-    x_ref, wf_ref, wq_ref, wkv_ref, wg_ref, wo_ref, wp_ref,
+    x_hbm, wf_hbm, wq_hbm, wkv_hbm, wg_hbm, wo_hbm, wp_hbm,
     update_out, pair_out,
-    normed_out, rows_in, factors_out, factors_in, rights, lefts, spread_q, w_turned, w_pair,
+    x_in, wf_ref, wq_ref, wkv_ref, wg_ref, wo_ref, wp_ref, normed_out, rows_in, factors_out, factors_in, rights, lefts, spread_q, w_turned, w_pair,
     update_made, aligned, held, blocks,
     f_send, f_recv, n_send, n_recv, x_send, x_recv, y_send, y_recv, w_send, w_recv,
-    l_send, l_recv, u_send, u_recv, p_send, p_recv, own_sem,
+    l_send, l_recv, u_send, u_recv, p_send, p_recv, own_sem, x_sem, weight_sem, v_send, v_recv,
 ):
+    def x_load(rel):
+        first = pl.multiple_of(seq_of(rel) * 8, 8)
+        return pltpu.make_async_copy(
+            x_hbm.at[:, pl.ds(first, 8), :], x_in.at[rel], x_sem.at[rel]
+        )
+
+    weight_loads = [
+        pltpu.make_async_copy(src, dst, weight_sem.at[n])
+        for n, (src, dst) in enumerate(
+            zip(
+                (wf_hbm, wq_hbm, wkv_hbm, wg_hbm, wo_hbm, wp_hbm),
+                (wf_ref, wq_ref, wkv_ref, wg_ref, wo_ref, wp_ref),
+            )
+        )
+    ]
+    x_load(2).start()
+    weight_loads[0].start()
+    for rel in (3, 1, 0):
+        x_load(rel).start()
+    for load in weight_loads[1:]:
+        load.start()
     barrier = pltpu.get_barrier_semaphore()
     partners = [seq_device(rel) for rel in (1, 2, 3)] + [x_device(1), x_device(-1)]
     partners += [gather_device(1), gather_device(-1)]
@@ -106,6 +127,13 @@
             rights.at[0, 0], rights.at[0, dx], x_send.at[dx - 1], x_recv.at[dx - 1], x_device(-dx)
         )
 
+    def x_relay(way):
+        half = pl.ds(16 * way, 16)
+        return remote(
+            rights.at[0, (1, 3)[way], half], rights.at[0, 2, half],
+            v_send.at[way], v_recv.at[way], x_device((-1, 1)[way]),
+        )
+
     def y_copy(dx, way):
         return remote(
             rights.at[0, dx], rights.at[(1, 3)[way], dx],
@@ -126,11 +154,10 @@
             lefts.at[0, 0], lefts.at[away, flip], l_send.at[n - 1], l_recv.at[n - 1], device
         )
 
-    def update_copy(rel, chunk):
-        part = pl.ds(chunk * PER_CHUNK, PER_CHUNK)
-        return remote(
-            update_made.at[rel, part], update_out.at[rel, part],
-            u_send.at[rel - 1, chunk], u_recv.at[rel - 1, chunk], seq_device(rel),
+    def update_copy(rel, r):
+        return remote(
+            update_made.at[rel, r], update_out.at[rel, r],
+            u_send.at[rel - 1, r], u_recv.at[rel - 1, r], seq_device(rel),
         )
 
     def block_copy(n):
@@ -141,19 +168,20 @@
             share_device(dz, dc),
         )
 
+    weight_loads[0].wait()
     weight = wf_ref[...]
     none = jnp.zeros_like(weight)
     even = jnp.concatenate([weight, none], axis=0)
     odd = jnp.concatenate([none, weight], axis=0)
     span = 32
     for rel in (2, 3, 1, 0):
-        first = pl.multiple_of(seq_of(rel) * 8, 8)
+        x_load(rel).wait()
         normed_ref = normed_out.at[rel - 1] if rel else rows_in.at[0]
         factor_ref = factors_out.at[rel - 1] if rel else factors_in.at[seq_of(0)]
 
-        def norm_rows(part, _, first=first, normed_ref=normed_ref):
+        def norm_rows(part, _, rel=rel, normed_ref=normed_ref):
             rows = pl.ds(pl.multiple_of(part * span, span), span)
-            x = x_ref[rows, pl.ds(first, 8), :].astype(F32)
+            x = x_in[rel, rows].astype(F32)
             centered = x - jnp.mean(x, axis=-1, keepdims=True)
             spread = jnp.mean(centered * centered, axis=-1, keepdims=True)
             normed = centered * lax.rsqrt(spread + epsilon)
@@ -170,30 +198,29 @@
             pl.semaphore_wait(barrier, len(partners))
         if rel:
             factor_copy(rel).start()
-    for rel in (1, 2, 3):
-        normed_copy(rel, 0).start()
-
+
+    for load in weight_loads[1:]:
+        load.wait()
     w_turned[:256] = wq_ref[...].astype(F32).T.astype(BF16)
     w_turned[256:512] = wkv_ref[:, 256:].astype(F32).T.astype(BF16)
     w_turned[512:] = wg_ref[...].astype(F32).T.astype(BF16)
     pair_rows = jnp.swapaxes(wp_ref[...].astype(F32).reshape(C, C, 128), 0, 1)
     w_pair[...] = pair_rows.reshape(C * C, 128).T.astype(BF16)
     spread_q[...] = jnp.zeros_like(spread_q)
+    for rel in (2, 3, 1):
+        normed_copy(rel, 0).start()
 
     for rel in (1, 2, 3):
         factor_copy(rel).wait_recv()
     turned = factors_in[...].astype(F32).reshape(384, 512).T.reshape(8, 64, 384)
     rights[0, 0] = jnp.swapaxes(turned[:, C:], 0, 1).astype(BF16)
     lefts[0, 0] = turned[:, :C].reshape(8 * C, 384).astype(BF16)
-    for dx in (1, 3, 2):
+    for dx in (1, 3):
         x_copy(dx).start()
     for way in (0, 1):
         y_copy(0, way).start()
     for n in range(1, 8):
         left_copy(n).start()
-    for chunk in range(1, CHUNKS):
-        for rel in (1, 2, 3):
-            normed_copy(rel, chunk).start()
 
     ones = jnp.ones((16, 384), BF16)
     scale = math.log2(math.e) / math.sqrt(HC)
@@ -234,43 +261,46 @@
     def chunk_step(chunk, _):
         for rel in (1, 2, 3):
             normed_copy(rel, chunk).wait_recv()
+        for before, ahead in ((0, 1), (1, 3)):
+
+            @pl.when(chunk == before)
+            def _(ahead=ahead):
+                for rel in (2, 3, 1):
+                    normed_copy(rel, ahead).start()
+
         for k in range(PER_CHUNK):
             residue(chunk * PER_CHUNK + k, k)
-        for rel in (1, 2, 3):
-            update_copy(rel, chunk).start()
-
         @pl.when(chunk == 0)
         def _():
+            for way in (0, 1):
+                x_copy((1, 3)[way]).wait_recv()
+                x_relay(way).start()
             for dx in (1, 3):
-                x_copy(dx).wait_recv()
                 for way in (0, 1):
                     y_copy(dx, way).start()
+            for rel in (2, 3, 1):
+                normed_copy(rel, 2).start()
+            for way in (0, 1):
+                x_relay(way).wait_recv()
+            for way in (0, 1):
+                y_copy(2, way).start()
             for way in (0, 1):
                 y_copy(0, way).wait_recv()
                 relay_copy(0, way).start()
-            x_copy(2).wait_recv()
-            for way in (0, 1):
-                y_copy(2, way).start()
 
         @pl.when(chunk == 1)
         def _():
-            for dx in (1, 3):
+            for dx in (1, 3, 2):
                 for way in (0, 1):
                     y_copy(dx, way).wait_recv()
                     relay_copy(dx, way).start()
 
-        @pl.when(chunk == 2)
-        def _():
-            for way in (0, 1):
-                y_copy(2, way).wait_recv()
-                relay_copy(2, way).start()
-
         return 0
 
-    lax.fori_loop(0, CHUNKS, chunk_step, 0)
-
-    own_update = pltpu.make_async_copy(update_made.at[0], update_out.at[0], own_sem.at[0])
-    own_update.start()
+    lax.fori_loop(0, CHUNKS - 1, chunk_step, 0)
+    for r in range(8 - PER_CHUNK):
+        for rel in (2, 3, 1):
+            update_copy(rel, r).start()
 
     for dx in range(4):
         for way in (0, 1):
@@ -286,35 +316,40 @@
     for n in range(1, 8):
         left_copy(n).wait_recv()
 
-    for dz in (2, 1, 3, 0):
-        left = lefts.at[dz]
-
-        def products(k, _, left=left):
-            right = aligned[pl.ds(2 * k, 2)].reshape(256, 384)
-            made = lax.dot_general(
-                left[...].reshape(512, 384), right, NT, preferred_element_type=F32
-            ).astype(BF16)
+    def share_tile(dz):
+        left = lefts[dz].reshape(512, 384)
+        for k in range(C // 2):
+            right = aligned[2 * k : 2 * k + 2].reshape(256, 384)
+            made = lax.dot_general(left, right, NT, preferred_element_type=F32).astype(BF16)
             for e in range(2):
-                at = pl.multiple_of((2 * k + e) * C, C)
-                held[:, pl.ds(at, C), :] = made[:, e * 128 : (e + 1) * 128].reshape(16, C, 128)
-            return 0
-
-        lax.fori_loop(0, C // 2, products, 0, unroll=4)
-        for dc in (0, 1):
-
-            def project(pair, _, dz=dz, dc=dc):
-                i = 8 * dc + 2 * pair
-                cols = jnp.concatenate([held[i], held[i + 1]], axis=1)
-                made = jnp.dot(w_pair[...], cols, preferred_element_type=F32) * (1.0 / 384)
-                for k in range(2):
-                    blocks[2 * dz + dc, 2 * pair + k] = (
-                        made[:, k * 128 : (k + 1) * 128].T.astype(BF16)
-                    )
-                return 0
-
-            lax.fori_loop(0, 4, project, 0, unroll=True)
-            if dz or dc:
-                block_copy(2 * dz + dc).start()
+                at = (2 * k + e) * C
+                held[:, at : at + C, :] = made[:, e * 128 : (e + 1) * 128].reshape(16, C, 128)
+        for pair in range(8):
+            cols = jnp.concatenate([held[2 * pair], held[2 * pair + 1]], axis=1)
+            made = jnp.dot(w_pair[...], cols, preferred_element_type=F32) * (1.0 / 384)
+            for k in range(2):
+                i = 2 * pair + k
+                blocks[2 * dz + i // 8, i % 8] = made[:, k * 128 : (k + 1) * 128].T.astype(BF16)
+        for n in (2 * dz, 2 * dz + 1):
+            if n:
+                block_copy(n).start()
+
+    for dz in (2, 1, 3):
+        share_tile(dz)
+
+    for rel in (1, 2, 3):
+        normed_copy(rel, CHUNKS - 1).wait_recv()
+
+    def last_residue(r, _):
+        residue(r, 0)
+        for rel in (2, 3, 1):
+            update_copy(rel, r).start()
+        return 0
+
+    lax.fori_loop(8 - PER_CHUNK, 8, last_residue, 0)
+    own_update = pltpu.make_async_copy(update_made.at[0], update_out.at[0], own_sem.at[0])
+    own_update.start()
+    share_tile(0)
     own_block = pltpu.make_async_copy(blocks.at[0], pair_out.at[0], own_sem.at[1])
     own_block.start()
 
@@ -322,9 +357,11 @@
         factor_copy(rel).wait_send()
         for chunk in range(CHUNKS):
             normed_copy(rel, chunk).wait_send()
-            update_copy(rel, chunk).wait()
-    for dx in (1, 2, 3):
-        x_copy(dx).wait_send()
+        for r in range(8):
+            update_copy(rel, r).wait()
+    for way in (0, 1):
+        x_copy((1, 3)[way]).wait_send()
+        x_relay(way).wait_send()
     for dx in range(4):
         for way in (0, 1):
             y_copy(dx, way).wait_send()
@@ -341,13 +378,20 @@
     dma = pltpu.SemaphoreType.DMA
     return pl.pallas_call(
         step_kernel,
-        in_specs=[VMEM_SPEC] * 7,
+        in_specs=[ANY_SPEC] * 7,
         out_specs=[ANY_SPEC] * 2,
         out_shape=[
             jax.ShapeDtypeStruct((4, 8, 96, 256), BF16),
             jax.ShapeDtypeStruct((8, 8, 128, 128), BF16),
         ],
         scratch_shapes=[
+            pltpu.VMEM((4, 96, 8, 256), BF16),
+            pltpu.VMEM((64, 256), BF16),
+            pltpu.VMEM((256, 256), BF16),
+            pltpu.VMEM((256, 512), BF16),
+            pltpu.VMEM((256, 256), BF16),
+            pltpu.VMEM((256, 256), BF16),
+            pltpu.VMEM((1024, 128), BF16),
             pltpu.VMEM((3, 8, 96, 256), BF16),
             pltpu.VMEM((4, 8, 96, 256), BF16),
             pltpu.VMEM((3, 96, 512), BF16),
@@ -363,7 +407,7 @@
             pltpu.VMEM((8, 8, 128, 128), BF16),
             dma((3,)), dma((3,)), dma((3, CHUNKS)), dma((3, CHUNKS)), dma((3,)), dma((3,)),
             dma((4, 2)), dma((4, 2)), dma((4, 2)), dma((4, 2)), dma((7,)), dma((7,)),
-            dma((3, CHUNKS)), dma((3, CHUNKS)), dma((7,)), dma((7,)), dma((2,)),
+            dma((3, 8)), dma((3, 8)), dma((7,)), dma((7,)), dma((2,)), dma((4,)), dma((6,)), dma((2,)), dma((2,)),
         ],
         compiler_params=pltpu.CompilerParams(
             collective_id=0, has_side_effects=True, vmem_limit_bytes=58 * 2**20

time: 72.2 us -> 65.5 us (0.907)
  Pallas kernels: 71.3 us -> 64.6 us
    pallas_call x1, Pallas kernels: 67.8 us -> 61.1 us  [step_call(): pl.pallas_call(step_kernel, in_specs=[ANY_SPEC] * 7, out_specs=[ANY_SPEC]...]
where the time goes in v2:
time: 65.5 us; the launch traced here: 65.4 us
  Pallas kernels  64.6 us (99%)
  between operations  0.82 us (1%)
    pallas_call x1, Pallas kernels, step_call(): pl.pallas_call(step_kernel, in_specs=[ANY_SPEC] * 7, out_specs=[ANY_SPEC]...  61.1 us
    pallas_call x1, Pallas kernels, place_call(): pl.pallas_call(place_kernel, in_specs=[ANY_SPEC] * 2, out_specs=[ANY_SPEC...  3.46 us

profile of v2, /device:TPU:1, one launch (start us, length us, event | category | flops | bytes accessed | tf_op | source)
XLA Modules:
  0.0 65.4 jit_solution(13409994439028525491)
XLA Ops:
  0.6 61.1 %step.1 = (bf16[4,8,96,256]{3,2,1,0:T(8,128)(2,1)}, bf16[8,8,128,128]{3,2,1,0:T(8,128)(2,1)}) custom-call(bf16[96,32,256]{2,1,0:T(8,128)(2,1)} %x_hbm.1, bf16[64,256]{1,0:T(8,128)(2,1)} %bitcast.4, bf16[256,256]{1,0:T(8,128)(2,1)} %wq_hbm.1, bf16[256,512]{1,0:T(8,128)(2,1)} %wkv_hbm.1, bf16[256,256]{1,0:T(8,128)(2,1)} %wg_hbm.1, bf16[256,256]{1,0:T(8,128)(2,1)} %wo_hbm.1, ...), custom_call_target="tpu_custom_call" | custom-call | tf_op jit(solution)/shard_map/step/pallas_call | solution.py:379
  61.7 3.5 %place.1 = (bf16[96,32,256]{2,1,0:T(8,128)(2,1)}, bf16[8,2,4,4,2,2,8,128]{7,6,5,4,3,2,1,0:T(8,128)(2,1)}) custom-call(bf16[4,8,96,256]{3,2,1,0:T(8,128)(2,1)} %get-tuple-element.6.update_ref, bf16[8,8,16,8,128]{4,3,2,1,0:T(8,128)(2,1)} %bitcast.3), custom_call_target="tpu_custom_call" | custom-call | tf_op jit(solution)/shard_map/place/pallas_call | solution.py:469

commit v3 on v2

--- a/solution.py
+++ b/solution.py
@@ -21,6 +21,7 @@
 RELS = ((0, 0), (0, 1), (1, 0), (1, 1))
 CHUNKS = 4
 PER_CHUNK = 8 // CHUNKS
+AHEAD = 2
 F32 = jnp.float32
 BF16 = jnp.bfloat16
 VMEM_SPEC = pl.BlockSpec(memory_space=pltpu.VMEM)
@@ -225,39 +226,64 @@
     ones = jnp.ones((16, 384), BF16)
     scale = math.log2(math.e) / math.sqrt(HC)
 
-    def residue(r, slot):
+    def project(r, slot):
         rows = jnp.concatenate([rows_in[k, r] for k in range(4)], axis=0)
+        queries = lax.dot_general(w_turned[:256], rows, NT, preferred_element_type=F32).astype(BF16)
+        for h in range(HEADS):
+            at = slice(h * HC, (h + 1) * HC)
+            spread_q[slot, h // 2, at, (h % 2) * 384 : (h % 2 + 1) * 384] = queries[at]
         keys = jnp.dot(rows, wkv_ref[:, :256], preferred_element_type=F32).astype(BF16)
-        queries = lax.dot_general(w_turned[:256], rows, NT, preferred_element_type=F32).astype(BF16)
         values = lax.dot_general(
             w_turned[256:512], rows, NT, preferred_element_type=F32
         ).astype(BF16)
         gating = jax.nn.sigmoid(
             lax.dot_general(w_turned[512:], rows, NT, preferred_element_type=F32)
         )
-        for h in range(HEADS):
+        return keys, values, gating
+
+    def score(made, slot, pair):
+        scores = jnp.dot(made[0], spread_q[slot, pair], preferred_element_type=F32)
+        return jnp.exp2(scores * scale).astype(BF16)
+
+    def gather_pair(made, weights, pair):
+        gated = []
+        for k in range(2):
+            h = 2 * pair + k
             at = slice(h * HC, (h + 1) * HC)
-            spread_q[slot, h // 2, at, (h % 2) * 384 : (h % 2 + 1) * 384] = queries[at]
-        gated = []
-        for pair in range(HEADS // 2):
-            scores = jnp.dot(keys, spread_q[slot, pair], preferred_element_type=F32)
-            weights = jnp.exp2(scores * scale).astype(BF16)
-            for k in range(2):
-                h = 2 * pair + k
-                at = slice(h * HC, (h + 1) * HC)
-                summed = jnp.dot(
-                    jnp.concatenate([values[at], ones], axis=0),
-                    weights[:, k * 384 : (k + 1) * 384],
-                    preferred_element_type=F32,
-                )
-                attended = summed[:HC] / summed[HC : HC + 1]
-                gated.append((gating[at] * attended).astype(BF16))
+            summed = jnp.dot(
+                jnp.concatenate([made[1][at], ones], axis=0),
+                weights[:, k * 384 : (k + 1) * 384],
+                preferred_element_type=F32,
+            )
+            attended = summed[:HC] / summed[HC : HC + 1]
+            gated.append((made[2][at] * attended).astype(BF16))
+        return gated
+
+    def finish(r, gated):
         update = lax.dot_general(
             jnp.concatenate(gated, axis=0), wo_ref[...], TN, preferred_element_type=F32
         ).astype(BF16)
         for k in range(4):
             update_made[k, r] = update[k * 96 : (k + 1) * 96]
 
+    def attend(rows):
+        waiting = []
+        gated = [[] for _ in rows]
+
+        def drain(left):
+            while len(waiting) > left:
+                n, made, weights, pair = waiting.pop(0)
+                gated[n].extend(gather_pair(made, weights, pair))
+                if len(gated[n]) == HEADS:
+                    finish(rows[n], gated[n])
+
+        for n, r in enumerate(rows):
+            made = project(r, n)
+            for pair in range(HEADS // 2):
+                waiting.append((n, made, score(made, n, pair), pair))
+                drain(AHEAD)
+        drain(0)
+
     def chunk_step(chunk, _):
         for rel in (1, 2, 3):
             normed_copy(rel, chunk).wait_recv()
@@ -268,8 +294,7 @@
                 for rel in (2, 3, 1):
                     normed_copy(rel, ahead).start()
 
-        for k in range(PER_CHUNK):
-            residue(chunk * PER_CHUNK + k, k)
+        attend([chunk * PER_CHUNK + k for k in range(PER_CHUNK)])
         @pl.when(chunk == 0)
         def _():
             for way in (0, 1):
@@ -341,7 +366,7 @@
         normed_copy(rel, CHUNKS - 1).wait_recv()
 
     def last_residue(r, _):
-        residue(r, 0)
+        attend([r])
         for rel in (2, 3, 1):
             update_copy(rel, r).start()
         return 0

time: 65.5 us -> 63.3 us (0.966)
  Pallas kernels: 64.6 us -> 62.4 us
    pallas_call x1, Pallas kernels: 61.1 us -> 58.9 us  [step_call(): pl.pallas_call(step_kernel, in_specs=[ANY_SPEC] * 7, out_specs=[ANY_SPEC]...]
where the time goes in v3:
time: 63.3 us; the launch traced here: 63.2 us
  Pallas kernels  62.4 us (99%)
  between operations  0.82 us (1%)
    pallas_call x1, Pallas kernels, step_call(): pl.pallas_call(step_kernel, in_specs=[ANY_SPEC] * 7, out_specs=[ANY_SPEC]...  58.9 us
    pallas_call x1, Pallas kernels, place_call(): pl.pallas_call(place_kernel, in_specs=[ANY_SPEC] * 2, out_specs=[ANY_SPEC...  3.46 us

profile of v3, /device:TPU:1, one launch (start us, length us, event | category | flops | bytes accessed | tf_op | source)
XLA Modules:
  0.0 63.2 jit_solution(14649858308506624638)
XLA Ops:
  0.6 58.9 %step.1 = (bf16[4,8,96,256]{3,2,1,0:T(8,128)(2,1)}, bf16[8,8,128,128]{3,2,1,0:T(8,128)(2,1)}) custom-call(bf16[96,32,256]{2,1,0:T(8,128)(2,1)} %x_hbm.1, bf16[64,256]{1,0:T(8,128)(2,1)} %bitcast.4, bf16[256,256]{1,0:T(8,128)(2,1)} %wq_hbm.1, bf16[256,512]{1,0:T(8,128)(2,1)} %wkv_hbm.1, bf16[256,256]{1,0:T(8,128)(2,1)} %wg_hbm.1, bf16[256,256]{1,0:T(8,128)(2,1)} %wo_hbm.1, ...), custom_call_target="tpu_custom_call" | custom-call | tf_op jit(solution)/shard_map/step/pallas_call | solution.py:404
  59.6 3.5 %place.1 = (bf16[96,32,256]{2,1,0:T(8,128)(2,1)}, bf16[8,2,4,4,2,2,8,128]{7,6,5,4,3,2,1,0:T(8,128)(2,1)}) custom-call(bf16[4,8,96,256]{3,2,1,0:T(8,128)(2,1)} %get-tuple-element.6.update_ref, bf16[8,8,16,8,128]{4,3,2,1,0:T(8,128)(2,1)} %bitcast.3), custom_call_target="tpu_custom_call" | custom-call | tf_op jit(solution)/shard_map/place/pallas_call | solution.py:494

commit v4 on v3

--- a/solution.py
+++ b/solution.py
@@ -79,7 +79,7 @@
     x_in, wf_ref, wq_ref, wkv_ref, wg_ref, wo_ref, wp_ref, normed_out, rows_in, factors_out, factors_in, rights, lefts, spread_q, w_turned, w_pair,
     update_made, aligned, held, blocks,
     f_send, f_recv, n_send, n_recv, x_send, x_recv, y_send, y_recv, w_send, w_recv,
-    l_send, l_recv, u_send, u_recv, p_send, p_recv, own_sem, x_sem, weight_sem, v_send, v_recv,
+    l_send, l_recv, u_send, u_recv, p_send, p_recv, own_sem, x_sem, weight_sem,
 ):
     def x_load(rel):
         first = pl.multiple_of(seq_of(rel) * 8, 8)
@@ -128,13 +128,6 @@
             rights.at[0, 0], rights.at[0, dx], x_send.at[dx - 1], x_recv.at[dx - 1], x_device(-dx)
         )
 
-    def x_relay(way):
-        half = pl.ds(16 * way, 16)
-        return remote(
-            rights.at[0, (1, 3)[way], half], rights.at[0, 2, half],
-            v_send.at[way], v_recv.at[way], x_device((-1, 1)[way]),
-        )
-
     def y_copy(dx, way):
         return remote(
             rights.at[0, dx], rights.at[(1, 3)[way], dx],
@@ -216,7 +209,7 @@
     turned = factors_in[...].astype(F32).reshape(384, 512).T.reshape(8, 64, 384)
     rights[0, 0] = jnp.swapaxes(turned[:, C:], 0, 1).astype(BF16)
     lefts[0, 0] = turned[:, :C].reshape(8 * C, 384).astype(BF16)
-    for dx in (1, 3):
+    for dx in (1, 3, 2):
         x_copy(dx).start()
     for way in (0, 1):
         y_copy(0, way).start()
@@ -287,7 +280,7 @@
     def chunk_step(chunk, _):
         for rel in (1, 2, 3):
             normed_copy(rel, chunk).wait_recv()
-        for before, ahead in ((0, 1), (1, 3)):
+        for before, ahead in ((0, 1), (2, 3)):
 
             @pl.when(chunk == before)
             def _(ahead=ahead):
@@ -299,26 +292,24 @@
         def _():
             for way in (0, 1):
                 x_copy((1, 3)[way]).wait_recv()
-                x_relay(way).start()
             for dx in (1, 3):
                 for way in (0, 1):
                     y_copy(dx, way).start()
+            x_copy(2).wait_recv()
+            for way in (0, 1):
+                y_copy(2, way).start()
             for rel in (2, 3, 1):
                 normed_copy(rel, 2).start()
-            for way in (0, 1):
-                x_relay(way).wait_recv()
-            for way in (0, 1):
-                y_copy(2, way).start()
-            for way in (0, 1):
-                y_copy(0, way).wait_recv()
-                relay_copy(0, way).start()
-
-        @pl.when(chunk == 1)
-        def _():
-            for dx in (1, 3, 2):
+            for dx in (0, 1, 3):
                 for way in (0, 1):
                     y_copy(dx, way).wait_recv()
                     relay_copy(dx, way).start()
+
+        @pl.when(chunk == 1)
+        def _():
+            for way in (0, 1):
+                y_copy(2, way).wait_recv()
+                relay_copy(2, way).start()
 
         return 0
 
@@ -384,9 +375,8 @@
             normed_copy(rel, chunk).wait_send()
         for r in range(8):
             update_copy(rel, r).wait()
-    for way in (0, 1):
-        x_copy((1, 3)[way]).wait_send()
-        x_relay(way).wait_send()
+    for dx in (1, 2, 3):
+        x_copy(dx).wait_send()
     for dx in range(4):
         for way in (0, 1):
             y_copy(dx, way).wait_send()
@@ -432,7 +422,7 @@
             pltpu.VMEM((8, 8, 128, 128), BF16),
             dma((3,)), dma((3,)), dma((3, CHUNKS)), dma((3, CHUNKS)), dma((3,)), dma((3,)),
             dma((4, 2)), dma((4, 2)), dma((4, 2)), dma((4, 2)), dma((7,)), dma((7,)),
-            dma((3, 8)), dma((3, 8)), dma((7,)), dma((7,)), dma((2,)), dma((4,)), dma((6,)), dma((2,)), dma((2,)),
+            dma((3, 8)), dma((3, 8)), dma((7,)), dma((7,)), dma((2,)), dma((4,)), dma((6,)),
         ],
         compiler_params=pltpu.CompilerParams(
             collective_id=0, has_side_effects=True, vmem_limit_bytes=58 * 2**20

time: 63.3 us -> 64.2 us (1.014)
  Pallas kernels: 62.4 us -> 63.2 us
    pallas_call x1, Pallas kernels: 58.9 us -> 59.8 us  [step_call(): pl.pallas_call(step_kernel, in_specs=[ANY_SPEC] * 7, out_specs=[ANY_SPEC]...]
where the time goes in v4:
time: 64.2 us; the launch traced here: 64 us
  Pallas kernels  63.2 us (98%)
  between operations  0.82 us (1%)
    pallas_call x1, Pallas kernels, step_call(): pl.pallas_call(step_kernel, in_specs=[ANY_SPEC] * 7, out_specs=[ANY_SPEC]...  59.8 us
    pallas_call x1, Pallas kernels, place_call(): pl.pallas_call(place_kernel, in_specs=[ANY_SPEC] * 2, out_specs=[ANY_SPEC...  3.46 us

profile of v4, /device:TPU:1, one launch (start us, length us, event | category | flops | bytes accessed | tf_op | source)
XLA Modules:
  0.0 64.0 jit_solution(2372148409454279688)
XLA Ops:
  0.6 59.8 %step.1 = (bf16[4,8,96,256]{3,2,1,0:T(8,128)(2,1)}, bf16[8,8,128,128]{3,2,1,0:T(8,128)(2,1)}) custom-call(bf16[96,32,256]{2,1,0:T(8,128)(2,1)} %x_hbm.1, bf16[64,256]{1,0:T(8,128)(2,1)} %bitcast.4, bf16[256,256]{1,0:T(8,128)(2,1)} %wq_hbm.1, bf16[256,512]{1,0:T(8,128)(2,1)} %wkv_hbm.1, bf16[256,256]{1,0:T(8,128)(2,1)} %wg_hbm.1, bf16[256,256]{1,0:T(8,128)(2,1)} %wo_hbm.1, ...), custom_call_target="tpu_custom_call" | custom-call | tf_op jit(solution)/shard_map/step/pallas_call | solution.py:394
  60.4 3.5 %place.1 = (bf16[96,32,256]{2,1,0:T(8,128)(2,1)}, bf16[8,2,4,4,2,2,8,128]{7,6,5,4,3,2,1,0:T(8,128)(2,1)}) custom-call(bf16[4,8,96,256]{3,2,1,0:T(8,128)(2,1)} %get-tuple-element.6.update_ref, bf16[8,8,16,8,128]{4,3,2,1,0:T(8,128)(2,1)} %bitcast.3), custom_call_target="tpu_custom_call" | custom-call | tf_op jit(solution)/shard_map/place/pallas_call | solution.py:484

commit v5 on v3

--- a/solution.py
+++ b/solution.py
@@ -287,7 +287,7 @@
     def chunk_step(chunk, _):
         for rel in (1, 2, 3):
             normed_copy(rel, chunk).wait_recv()
-        for before, ahead in ((0, 1), (1, 3)):
+        for before, ahead in ((0, 1), (2, 3)):
 
             @pl.when(chunk == before)
             def _(ahead=ahead):
@@ -315,10 +315,16 @@
 
         @pl.when(chunk == 1)
         def _():
-            for dx in (1, 3, 2):
+            for dx in (1, 3):
                 for way in (0, 1):
                     y_copy(dx, way).wait_recv()
                     relay_copy(dx, way).start()
+
+        @pl.when(chunk == 2)
+        def _():
+            for way in (0, 1):
+                y_copy(2, way).wait_recv()
+                relay_copy(2, way).start()
 
         return 0
 

time: 63.3 us -> 64.5 us (1.019)
  Pallas kernels: 62.4 us -> 63.5 us
    pallas_call x1, Pallas kernels: 58.9 us -> 60.1 us  [step_call(): pl.pallas_call(step_kernel, in_specs=[ANY_SPEC] * 7, out_specs=[ANY_SPEC]...]
where the time goes in v5:
time: 64.5 us; the launch traced here: 64.4 us
  Pallas kernels  63.5 us (98%)
  between operations  0.82 us (1%)
    pallas_call x1, Pallas kernels, step_call(): pl.pallas_call(step_kernel, in_specs=[ANY_SPEC] * 7, out_specs=[ANY_SPEC]...  60.1 us
    pallas_call x1, Pallas kernels, place_call(): pl.pallas_call(place_kernel, in_specs=[ANY_SPEC] * 2, out_specs=[ANY_SPEC...  3.46 us

profile of v5, /device:TPU:1, one launch (start us, length us, event | category | flops | bytes accessed | tf_op | source)
XLA Modules:
  0.0 64.4 jit_solution(14323682613738611383)
XLA Ops:
  0.6 60.1 %step.1 = (bf16[4,8,96,256]{3,2,1,0:T(8,128)(2,1)}, bf16[8,8,128,128]{3,2,1,0:T(8,128)(2,1)}) custom-call(bf16[96,32,256]{2,1,0:T(8,128)(2,1)} %x_hbm.1, bf16[64,256]{1,0:T(8,128)(2,1)} %bitcast.4, bf16[256,256]{1,0:T(8,128)(2,1)} %wq_hbm.1, bf16[256,512]{1,0:T(8,128)(2,1)} %wkv_hbm.1, bf16[256,256]{1,0:T(8,128)(2,1)} %wg_hbm.1, bf16[256,256]{1,0:T(8,128)(2,1)} %wo_hbm.1, ...), custom_call_target="tpu_custom_call" | custom-call | tf_op jit(solution)/shard_map/step/pallas_call | solution.py:410
  60.7 3.5 %place.1 = (bf16[96,32,256]{2,1,0:T(8,128)(2,1)}, bf16[8,2,4,4,2,2,8,128]{7,6,5,4,3,2,1,0:T(8,128)(2,1)}) custom-call(bf16[4,8,96,256]{3,2,1,0:T(8,128)(2,1)} %get-tuple-element.6.update_ref, bf16[8,8,16,8,128]{4,3,2,1,0:T(8,128)(2,1)} %bitcast.3), custom_call_target="tpu_custom_call" | custom-call | tf_op jit(solution)/shard_map/place/pallas_call | solution.py:500
